TPU v7x, 32 devices: a whole 2x2x4 slice. The times are simulated.
32 devices in a mesh: group: 2 (over x), tensor: 16 (over z, y, core).
Axes of the slice: x: 2, y: 2, z: 4, core: 2. Of those that a mesh axis runs over, the one named last changes fastest.
Arguments:
- z_star: bfloat16 [64, 5120], P(('group', 'tensor')), parts along dimension 0, may hold values from -6 to 6
- grad_out: float32 [64, 5120], P(('group', 'tensor')), parts along dimension 0, may hold values from -30 to 30
- w_gate: bfloat16 [10240, 13824], P('group', 'tensor'), parts along dimension 0, may hold values from -0.078125 to 0.078125
- w_up: bfloat16 [10240, 13824], P('group', 'tensor'), parts along dimension 0, may hold values from -0.078125 to 0.078125
- w_down: bfloat16 [27648, 5120], P(('group', 'tensor')), parts along dimension 0, may hold values from -0.0546875 to 0.0546875
- norm_gain: float32 [10240], P('group'), parts along dimension 0, may hold values from 0.5 to 1.5
- mix_rate: float32 [10240], P('group'), parts along dimension 0, may hold values from 0.3 to 1
Outputs:
- adjoint: float32 [64, 5120], P(('group', 'tensor')), parts along dimension 0
- grad_gate: bfloat16 [10240, 13824], P('group', 'tensor'), parts along dimension 0
- grad_up: bfloat16 [10240, 13824], P('group', 'tensor'), parts along dimension 0
- grad_down: bfloat16 [27648, 5120], P(('group', 'tensor')), parts along dimension 0
There are 2 independent parts, one for each index of `group`. A program takes and returns all parts, laid end to end along the dimension named above; each array names one. Nothing has to cross between parts.
All inputs are finite; a program needn't handle non-finite values.
Results may differ from a plain program's by a relative error of at most 0.014.
Values may be sent and summed in bfloat16 or wider, within the bound.
No kernel may reach another device: no remote copies, remote signals or barrier semaphores. Data moves between devices by JAX's collectives and lax.ppermute only.
A program may use at most 128 MiB of HBM per device.

v0:
```python
import jax
import jax.numpy as jnp
from jax import lax
from jax.sharding import PartitionSpec as P


def contract(left, right, left_dim, right_dim):
    return lax.dot_general(
        left, right, (((left_dim,), (right_dim,)), ((), ())), preferred_element_type=jnp.float32
    )


def normalize(z_rows, norm_gain):
    values = z_rows.astype(jnp.float32)
    root_mean = jnp.sqrt(jnp.mean(values * values, axis=-1, keepdims=True) + 1e-06)
    unit_rows = values / root_mean
    normed = (unit_rows * norm_gain).astype(jnp.bfloat16)
    return (root_mean, unit_rows, normed)


def norm_back(normed_grad, norm_gain, unit_rows, root_mean):
    scaled = norm_gain * normed_grad
    return (scaled - unit_rows * jnp.mean(scaled * unit_rows, axis=-1, keepdims=True)) / root_mean


def body(z_star, grad_out, w_gate, w_up, w_down, norm_gain, mix_rate):
    local_rows = z_star.shape[0]
    z_full = lax.all_gather(z_star, "tensor", axis=0, tiled=True)
    root_mean, unit_rows, normed = normalize(z_full, norm_gain)
    gate_pre = contract(normed, w_gate, 1, 0)
    lifted = contract(normed, w_up, 1, 0)
    sigma = jax.nn.sigmoid(gate_pre)
    gated = gate_pre * sigma
    slope = sigma * (1.0 + gate_pre * (1.0 - sigma))
    hidden = (gated * lifted).astype(jnp.bfloat16)

    def branch_rows(state_half):
        hidden_grad = contract(state_half, w_down, 1, 1)
        gate_grad = (hidden_grad * lifted * slope).astype(jnp.bfloat16)
        lift_grad = (hidden_grad * gated).astype(jnp.bfloat16)
        return (gate_grad, lift_grad)

    cotangent = lax.all_gather(grad_out.astype(jnp.bfloat16), "tensor", axis=0, tiled=True).astype(
        grad_out.dtype
    )

    def jacobian(state):
        gate_grad, lift_grad = branch_rows(state.astype(jnp.bfloat16))
        partial_sum = contract(gate_grad, w_gate, 1, 1) + contract(lift_grad, w_up, 1, 1)
        normed_grad = lax.psum(partial_sum, "tensor")
        return norm_back(normed_grad, norm_gain, unit_rows, root_mean)

    resid_zero = jacobian(cotangent)
    state_one = cotangent + mix_rate * resid_zero
    resid_one = cotangent + jacobian(state_one) - state_one
    resid_diff = resid_one - resid_zero
    blend = jnp.sum(resid_one * resid_diff) / (jnp.sum(resid_diff * resid_diff) + 1e-06)
    adjoint = (
        state_one - blend * (state_one - cotangent) + mix_rate * (resid_one - blend * resid_diff)
    )
    adjoint_half = adjoint.astype(jnp.bfloat16)
    gate_grad, lift_grad = branch_rows(adjoint_half)
    grad_gate = contract(normed, gate_grad, 0, 0)
    grad_up = contract(normed, lift_grad, 0, 0)
    grad_down = contract(hidden, adjoint_half, 0, 0)
    adjoint_own = lax.dynamic_slice_in_dim(
        adjoint, lax.axis_index("tensor") * local_rows, local_rows, 0
    )
    return (
        adjoint_own,
        grad_gate.astype(jnp.bfloat16),
        grad_up.astype(jnp.bfloat16),
        grad_down.astype(jnp.bfloat16),
    )


def solution(mesh):
    placed = (
        P(("group", "tensor"), None),
        P(("group", "tensor"), None),
        P("group", "tensor"),
        P("group", "tensor"),
        P(("group", "tensor"), None),
        P("group"),
        P("group"),
    )
    return jax.shard_map(
        body,
        mesh=mesh,
        in_specs=placed,
        out_specs=(
            P(("group", "tensor"), None),
            P("group", "tensor"),
            P("group", "tensor"),
            P(("group", "tensor"), None),
        ),
        check_vma=False,
    )
```

profile of v0, /device:TPU:0, one launch (start us, length us, event | category | flops | bytes accessed | tf_op | source)
XLA Modules:
  0.0 303.7 jit_solution(8700253727963858324)
XLA Ops:
  7.2 0.0 all-reduce.3.cloned.1.call-start
  7.2 0.8 convert_bitcast_fusion
  8.0 24.0 %all-gather = bf16[16,2,5120]{2,1,0:T(2,128)(2,1)S(1)} all-gather(bf16[1,2,5120]{2,1,0:T(2,128)(2,1)S(1)} %convert_bitcast_fusion), channel_id=1, replica_groups=mesh['group'=2,'tensor'=16] {'tensor'}, dimensions={0}, use_global_device_ids=true | all-gather | bytes 348160 | tf_op jit(solution)/shard_map/all_gather | solution.py:43
  32.0 0.1 reshape.27
  32.2 18.6 %all-gather.1 = bf16[16,2,5120]{2,1,0:T(2,128)(2,1)S(1)} all-gather(bf16[1,2,5120]{2,1,0:T(2,128)(2,1)} %bitcast.21), channel_id=1, replica_groups=mesh['group'=2,'tensor'=16] {'tensor'}, dimensions={0}, use_global_device_ids=true | all-gather | bytes 348160 | tf_op jit(solution)/shard_map/all_gather | solution.py:28
  50.7 0.1 reshape.30
  50.8 0.2 multiply_reduce_fusion.4
  51.0 1.0 multiply_convert_fusion
  52.1 6.6 %fusion.21 = f32[32,864]{1,0:T(8,128)S(1)} fusion(bf16[32,5120]{1,0:T(8,128)(2,1)S(1)} %multiply_convert_fusion, bf16[5120,864]{0,1:T(8,128)(2,1)} %param.9), kind=kOutput, calls=%fused_computation.45 | convolution fusion | flops 283115520 | bytes 9285632 | tf_op jit(solution)/shard_map/dot_general | solution.py:8
  58.7 0.0 slice-start
  58.8 2.7 fusion.20
  61.4 0.0 slice-start.2
  61.4 2.7 fusion.19
  64.1 0.0 slice-done.1
  64.2 1.6 fusion.12
  65.8 2.5 convolution_add_fusion.1
  68.3 0.2 all-reduce.5.cloned.1.call-start
  68.5 90.0 %all-reduce.3.cloned.1.call-done = f32[32,5120]{1,0:T(8,128)} async-done(((f32[32,5120]{1,0:T(8,128)}), f32[32,5120]{1,0:T(8,128)}) %all-reduce.3.cloned.1.call-update) | async-done | bytes 655376 | tf_op jit(solution)/shard_map/psum | solution.py:50
  158.5 1.3 multiply_reduce_fusion.3
  159.8 1.3 subtract_divide_fusion
  161.1 6.3 %fusion.5 = f32[32,864]{1,0:T(8,128)S(1)} fusion(bf16[864,5120]{1,0:T(8,128)(2,1)} %param.11, f32[32,5120]{1,0:T(8,128)S(1)} %subtract_divide_fusion, bf16[32,5120]{1,0:T(8,128)(2,1)S(1)} %reshape.27, f32[5120]{0:T(1024)S(1)} %copy-done.3), kind=kOutput, calls=%fused_computation.20 | convolution fusion | flops 283770880 | bytes 9961472 | tf_op jit(solution)/shard_map/dot_general | solution.py:8
  167.5 5.3 %fusion.13 = f32[32,5120]{1,0:T(8,128)S(1)} fusion(bf16[5120,864]{0,1:T(8,128)(2,1)} %param.9, f32[32,864]{1,0:T(8,128)S(1)} %fusion.5, f32[32,864]{1,0:T(8,128)S(1)} %fusion.20, f32[32,864]{1,0:T(8,128)S(1)} %fusion.21), kind=kOutput, calls=%fused_computation.37 | convolution fusion | flops 283392000 | bytes 9834496 | tf_op jit(solution)/shard_map/dot_general | solution.py:8
  172.8 2.5 convolution_add_fusion
  175.3 91.6 %all-reduce.5.cloned.1.call-done = f32[32,5120]{1,0:T(8,128)} async-done(((f32[32,5120]{1,0:T(8,128)}), f32[32,5120]{1,0:T(8,128)}) %all-reduce.5.cloned.1.call-update) | async-done | bytes 655376 | tf_op jit(solution)/shard_map/psum | solution.py:50
  266.9 1.3 multiply_reduce_fusion.2
  268.2 2.1 multiply_reduce_fusion
  271.6 0.2 fusion.3
  271.8 6.1 %fusion.9 = f32[32,864]{1,0:T(8,128)S(1)} fusion(bf16[864,5120]{1,0:T(8,128)(2,1)} %param.11, f32[32,5120]{1,0:T(8,128)S(1)} %fusion.3), kind=kOutput, calls=%fused_computation.24 | convolution fusion | flops 283279360 | bytes 9613312 | tf_op jit(solution)/shard_map/dot_general | solution.py:8
  278.0 6.1 %convolution_convert_fusion = bf16[864,5120]{1,0:T(8,128)(2,1)} fusion(f32[32,5120]{1,0:T(8,128)S(1)} %fusion.3, f32[32,864]{1,0:T(8,128)S(1)} %fusion.20, f32[32,864]{1,0:T(8,128)S(1)} %fusion.21), kind=kOutput, calls=%fused_computation | convolution fusion | flops 287868928 | bytes 9723904 | tf_op jit(solution)/shard_map/dot_general | solution.py:8
  284.1 6.1 %convolution_convert_fusion.2 = bf16[5120,864]{0,1:T(8,128)(2,1)} fusion(bf16[32,5120]{1,0:T(8,128)(2,1)S(1)} %multiply_convert_fusion, f32[32,864]{1,0:T(8,128)S(1)} %fusion.9, f32[32,864]{1,0:T(8,128)S(1)} %fusion.20, f32[32,864]{1,0:T(8,128)S(1)} %fusion.21), kind=kOutput, calls=%fused_computation.2 | convolution fusion | flops 287815680 | bytes 9506816 | tf_op jit(solution)/shard_map/dot_general | solution.py:8
  290.1 6.1 %convolution_convert_fusion.1 = bf16[5120,864]{0,1:T(8,128)(2,1)} fusion(bf16[32,5120]{1,0:T(8,128)(2,1)S(1)} %multiply_convert_fusion, f32[32,864]{1,0:T(8,128)S(1)} %fusion.9, f32[32,864]{1,0:T(8,128)S(1)} %fusion.21), kind=kOutput, calls=%fused_computation.1 | convolution fusion | flops 287705088 | bytes 9396224 | tf_op jit(solution)/shard_map/dot_general | solution.py:8
  296.2 0.6 constant_dynamic-slice_fusion
  (24 shorter events, 0.1 us)
Async XLA Ops:
  7.2 151.3 %all-reduce.3.cloned.1.call-start = ((), (), s32[]{:S(2)}) async-start(), calls=%async_computation | async-start | bytes 1310720 | tf_op jit(solution)/shard_map/psum | solution.py:50
  50.8 7.9 %copy-start = (bf16[5120,864]{0,1:T(8,128)(2,1)S(1)}, bf16[5120,864]{0,1:T(8,128)(2,1)}, u32[]{:S(2)}) copy-start(bf16[5120,864]{0,1:T(8,128)(2,1)} %param.10) | copy-start | bytes 26542084
  52.0 9.4 %copy-start.1 = (bf16[864,5120]{1,0:T(8,128)(2,1)S(1)}, bf16[864,5120]{1,0:T(8,128)(2,1)}, u32[]{:S(2)}) copy-start(bf16[864,5120]{1,0:T(8,128)(2,1)} %param.11) | copy-start | bytes 26542084
  58.7 5.4 %slice-start = ((s8[8847360]{0:T(1024)(128)(4,1)}), s8[4194304]{0:T(1024)(128)(4,1)S(1)}, s32[]{:S(2)}) async-start(s8[8847360]{0:T(1024)(128)(4,1)} %bitcast.17), calls=%async_computation.2 | async-start | bytes 8388608
  58.7 5.4 %slice-start.1 = ((s8[8847360]{0:T(1024)(128)(4,1)}), s8[4194304]{0:T(1024)(128)(4,1)S(1)}, s32[]{:S(2)}) async-start(s8[8847360]{0:T(1024)(128)(4,1)} %bitcast.17), calls=%async_computation.3 | async-start | bytes 8388608
  61.4 2.7 slice-start.2
  65.8 92.7 %copy-start.2 = (f32[5120]{0:T(1024)S(1)}, f32[5120]{0:T(1024)}, u32[]{:S(2)}) copy-start(f32[5120]{0:T(1024)} %param.12) | copy-start | bytes 61444
  65.8 95.3 %copy-start.3 = (f32[5120]{0:T(1024)S(1)}, f32[5120]{0:T(1024)}, u32[]{:S(2)}) copy-start(f32[5120]{0:T(1024)} %param.13) | copy-start | bytes 61444
  68.3 198.6 %all-reduce.5.cloned.1.call-start = ((), (), s32[]{:S(2)}) async-start(), calls=%async_computation.1 | async-start | bytes 1310720 | tf_op jit(solution)/shard_map/psum | solution.py:50
  161.1 11.6 %slice-start.3 = ((s8[8847360]{0:T(1024)(128)(4,1)}), s8[4194304]{0:T(1024)(128)(4,1)S(1)}, s32[]{:S(2)}) async-start(s8[8847360]{0:T(1024)(128)(4,1)} %bitcast.19), calls=%async_computation.5 | async-start | bytes 8388608
  161.1 11.6 %slice-start.4 = ((s8[8847360]{0:T(1024)(128)(4,1)}), s8[458752]{0:T(1024)(128)(4,1)S(1)}, s32[]{:S(2)}) async-start(s8[8847360]{0:T(1024)(128)(4,1)} %bitcast.19), calls=%async_computation.6 | async-start | bytes 917504
  167.5 5.3 %slice-start.5 = ((s8[8847360]{0:T(1024)(128)(4,1)}), s8[4194304]{0:T(1024)(128)(4,1)S(1)}, s32[]{:S(2)}) async-start(s8[8847360]{0:T(1024)(128)(4,1)} %bitcast.19), calls=%async_computation.7 | async-start | bytes 8388608
Sparse Core Ops, SparseCore 0:
  68.4 90.0 all-reduce.2
  175.4 91.4 all-reduce.4
where the time goes:
time: 304 us
  waiting for transfers between devices  182 us (60%)
  matrix products  54.4 us (18%)
  blocking collectives  42.6 us (14%)
  between operations  15.5 us (5%)
  other arithmetic  8.24 us (3%)
    psum x2, waiting for transfers between devices, jacobian(): normed_grad = lax.psum(partial_sum, 'tensor')  182 us
    dot_general x12, matrix products, contract(): lax.dot_general(left, right, (((left_dim,), (right_dim,)), ((), ())), pre...  54.4 us
    all_gather x1, blocking collectives, body(): lax.all_gather(grad_out.astype(jnp.bfloat16), 'tensor', axis=0, tiled=True)  24 us
    all_gather x1, blocking collectives, body(): z_full = lax.all_gather(z_star, 'tensor', axis=0, tiled=True)  18.6 us
  transfers between devices with their start and end apart: 2, of which 2 were waited for; matrix products, arithmetic and copies ran while one was open for 0% of the time, Pallas kernels for 0%

commit v1 on v0

--- a/solution.py
+++ b/solution.py
@@ -2,6 +2,19 @@
 import jax.numpy as jnp
 from jax import lax
 from jax.sharding import PartitionSpec as P
+
+
+def gather_around(array, axis, dim):
+    devices, position, rows = (lax.axis_size(axis), lax.axis_index(axis), array.shape[dim])
+    right = [(i, (i + 1) % devices) for i in range(devices)]
+    filled = jnp.zeros((*array.shape[:dim], devices * rows, *array.shape[dim + 1 :]), array.dtype)
+    carried = array
+    for step in range(devices):
+        owner = (position - step) % devices
+        filled = lax.dynamic_update_slice_in_dim(filled, carried, owner * rows, axis=dim)
+        if step < devices - 1:
+            carried = lax.ppermute(carried, axis, right)
+    return filled
 
 
 def contract(left, right, left_dim, right_dim):
@@ -25,7 +38,7 @@
 
 def body(z_star, grad_out, w_gate, w_up, w_down, norm_gain, mix_rate):
     local_rows = z_star.shape[0]
-    z_full = lax.all_gather(z_star, "tensor", axis=0, tiled=True)
+    z_full = gather_around(z_star, "tensor", 0)
     root_mean, unit_rows, normed = normalize(z_full, norm_gain)
     gate_pre = contract(normed, w_gate, 1, 0)
     lifted = contract(normed, w_up, 1, 0)

time: 304 us -> 369 us (1.21)
  waiting for transfers between devices: 182 us -> 262 us
  blocking collectives: 42.6 us -> 23.6 us
    ppermute x0 -> x15, waiting for transfers between devices: none -> 81.8 us  [gather_around(): carried = lax.ppermute(carried, axis, right)]
    all_gather x1 -> x0, blocking collectives: 18.6 us -> none  [body(): z_full = lax.all_gather(z_star, 'tensor', axis=0, tiled=True)]
  transfers between devices with their start and end apart: 2 -> 17, of which waited for: 2 -> 16; matrix products, arithmetic and copies ran while one was open for 0% -> 2% of each run, Pallas kernels for 0% -> 0%
where the time goes in v1:
time: 369 us
  waiting for transfers between devices  262 us (71%)
  matrix products  57.9 us (16%)
  blocking collectives  23.6 us (6%)
  between operations  16 us (4%)
  other arithmetic  6.31 us (2%)
    psum x2, waiting for transfers between devices, jacobian(): normed_grad = lax.psum(partial_sum, 'tensor')  181 us
    ppermute x15, waiting for transfers between devices, gather_around(): carried = lax.ppermute(carried, axis, right)  81.8 us
    dot_general x12, matrix products, contract(): lax.dot_general(left, right, (((left_dim,), (right_dim,)), ((), ())), pre...  57.9 us
    all_gather x1, blocking collectives, body(): lax.all_gather(grad_out.astype(jnp.bfloat16), 'tensor', axis=0, tiled=True)  23.6 us
  transfers between devices with their start and end apart: 17, of which 16 were waited for; matrix products, arithmetic and copies ran while one was open for 2% of the time, Pallas kernels for 0%

profile of v1, /device:TPU:0, one launch (start us, length us, event | category | flops | bytes accessed | tf_op | source)
XLA Modules:
  0.0 368.7 jit_solution(9670303433625978515)
XLA Ops:
  8.6 23.6 %all-gather = bf16[16,2,5120]{2,1,0:T(2,128)(2,1)S(1)} all-gather(bf16[1,2,5120]{2,1,0:T(2,128)(2,1)S(1)} %convert_bitcast_fusion), channel_id=1, replica_groups=mesh['group'=2,'tensor'=16] {'tensor'}, dimensions={0}, use_global_device_ids=true | all-gather | bytes 348160 | tf_op jit(solution)/shard_map/all_gather | solution.py:56
  32.3 6.1 %fusion.24 = f32[32,864]{1,0:T(8,128)S(1)} fusion(bf16[32,5120]{1,0:T(8,128)(2,1)S(1)} %reshape.27, bf16[864,5120]{1,0:T(8,128)(2,1)} %param.11), kind=kOutput, calls=%fused_computation.63 | convolution fusion | flops 283115520 | bytes 9285632 | tf_op jit(solution)/shard_map/dot_general | solution.py:21
  39.3 5.5 %collective-permute-done.1 = bf16[2,5120]{1,0:T(2,128)(2,1)S(1)} collective-permute-done((bf16[2,5120]{1,0:T(2,128)(2,1)S(1)}, bf16[2,5120]{1,0:T(2,128)(2,1)S(1)}, u32[]{:S(2)}, u32[]{:S(2)}) %collective-permute-start.1) | collective-permute-done | bytes 20512 | tf_op jit(solution)/shard_map/ppermute | solution.py:16
  44.9 5.9 %collective-permute-done.2 = bf16[2,5120]{1,0:T(2,128)(2,1)S(1)} collective-permute-done((bf16[2,5120]{1,0:T(2,128)(2,1)S(1)}, bf16[2,5120]{1,0:T(2,128)(2,1)S(1)}, u32[]{:S(2)}, u32[]{:S(2)}) %collective-permute-start.2) | collective-permute-done | bytes 20512 | tf_op jit(solution)/shard_map/ppermute | solution.py:16
  50.8 5.9 %collective-permute-done.3 = bf16[2,5120]{1,0:T(2,128)(2,1)S(1)} collective-permute-done((bf16[2,5120]{1,0:T(2,128)(2,1)S(1)}, bf16[2,5120]{1,0:T(2,128)(2,1)S(1)}, u32[]{:S(2)}, u32[]{:S(2)}) %collective-permute-start.3) | collective-permute-done | bytes 20512 | tf_op jit(solution)/shard_map/ppermute | solution.py:16
  56.7 5.9 %collective-permute-done.4 = bf16[2,5120]{1,0:T(2,128)(2,1)S(1)} collective-permute-done((bf16[2,5120]{1,0:T(2,128)(2,1)S(1)}, bf16[2,5120]{1,0:T(2,128)(2,1)S(1)}, u32[]{:S(2)}, u32[]{:S(2)}) %collective-permute-start.4) | collective-permute-done | bytes 20512 | tf_op jit(solution)/shard_map/ppermute | solution.py:16
  62.6 5.9 %collective-permute-done.5 = bf16[2,5120]{1,0:T(2,128)(2,1)S(1)} collective-permute-done((bf16[2,5120]{1,0:T(2,128)(2,1)S(1)}, bf16[2,5120]{1,0:T(2,128)(2,1)S(1)}, u32[]{:S(2)}, u32[]{:S(2)}) %collective-permute-start.5) | collective-permute-done | bytes 20512 | tf_op jit(solution)/shard_map/ppermute | solution.py:16
  68.5 5.9 %collective-permute-done.6 = bf16[2,5120]{1,0:T(2,128)(2,1)S(1)} collective-permute-done((bf16[2,5120]{1,0:T(2,128)(2,1)S(1)}, bf16[2,5120]{1,0:T(2,128)(2,1)S(1)}, u32[]{:S(2)}, u32[]{:S(2)}) %collective-permute-start.6) | collective-permute-done | bytes 20512 | tf_op jit(solution)/shard_map/ppermute | solution.py:16
  74.4 5.9 %collective-permute-done.7 = bf16[2,5120]{1,0:T(2,128)(2,1)S(1)} collective-permute-done((bf16[2,5120]{1,0:T(2,128)(2,1)S(1)}, bf16[2,5120]{1,0:T(2,128)(2,1)S(1)}, u32[]{:S(2)}, u32[]{:S(2)}) %collective-permute-start.7) | collective-permute-done | bytes 20512 | tf_op jit(solution)/shard_map/ppermute | solution.py:16
  80.3 5.9 %collective-permute-done.8 = bf16[2,5120]{1,0:T(2,128)(2,1)S(1)} collective-permute-done((bf16[2,5120]{1,0:T(2,128)(2,1)S(1)}, bf16[2,5120]{1,0:T(2,128)(2,1)S(1)}, u32[]{:S(2)}, u32[]{:S(2)}) %collective-permute-start.8) | collective-permute-done | bytes 20512 | tf_op jit(solution)/shard_map/ppermute | solution.py:16
  86.2 5.9 %collective-permute-done.9 = bf16[2,5120]{1,0:T(2,128)(2,1)S(1)} collective-permute-done((bf16[2,5120]{1,0:T(2,128)(2,1)S(1)}, bf16[2,5120]{1,0:T(2,128)(2,1)S(1)}, u32[]{:S(2)}, u32[]{:S(2)}) %collective-permute-start.9) | collective-permute-done | bytes 20512 | tf_op jit(solution)/shard_map/ppermute | solution.py:16
  92.1 5.9 %collective-permute-done.10 = bf16[2,5120]{1,0:T(2,128)(2,1)S(1)} collective-permute-done((bf16[2,5120]{1,0:T(2,128)(2,1)S(1)}, bf16[2,5120]{1,0:T(2,128)(2,1)S(1)}, u32[]{:S(2)}, u32[]{:S(2)}) %collective-permute-start.10) | collective-permute-done | bytes 20512 | tf_op jit(solution)/shard_map/ppermute | solution.py:16
  98.0 5.9 %collective-permute-done.11 = bf16[2,5120]{1,0:T(2,128)(2,1)S(1)} collective-permute-done((bf16[2,5120]{1,0:T(2,128)(2,1)S(1)}, bf16[2,5120]{1,0:T(2,128)(2,1)S(1)}, u32[]{:S(2)}, u32[]{:S(2)}) %collective-permute-start.11) | collective-permute-done | bytes 20512 | tf_op jit(solution)/shard_map/ppermute | solution.py:16
  103.9 5.9 %collective-permute-done.12 = bf16[2,5120]{1,0:T(2,128)(2,1)S(1)} collective-permute-done((bf16[2,5120]{1,0:T(2,128)(2,1)S(1)}, bf16[2,5120]{1,0:T(2,128)(2,1)S(1)}, u32[]{:S(2)}, u32[]{:S(2)}) %collective-permute-start.12) | collective-permute-done | bytes 20512 | tf_op jit(solution)/shard_map/ppermute | solution.py:16
  109.8 5.9 %collective-permute-done.13 = bf16[2,5120]{1,0:T(2,128)(2,1)S(1)} collective-permute-done((bf16[2,5120]{1,0:T(2,128)(2,1)S(1)}, bf16[2,5120]{1,0:T(2,128)(2,1)S(1)}, u32[]{:S(2)}, u32[]{:S(2)}) %collective-permute-start.13) | collective-permute-done | bytes 20512 | tf_op jit(solution)/shard_map/ppermute | solution.py:16
  115.7 5.9 %collective-permute-done.14 = bf16[2,5120]{1,0:T(2,128)(2,1)S(1)} collective-permute-done((bf16[2,5120]{1,0:T(2,128)(2,1)S(1)}, bf16[2,5120]{1,0:T(2,128)(2,1)S(1)}, u32[]{:S(2)}, u32[]{:S(2)}) %collective-permute-start.14) | collective-permute-done | bytes 20512 | tf_op jit(solution)/shard_map/ppermute | solution.py:16
  121.9 6.3 %fusion.19 = f32[32,864]{1,0:T(8,128)S(1)} fusion(bf16[5120,864]{0,1:T(8,128)(2,1)} %param.9, f32[5120]{0:T(1024)S(1)} %copy-done.2, f32[32]{0:T(128)S(1)} %add_sqrt_fusion, bf16[32,5120]{1,0:T(8,128)(2,1)S(1)} %constant_dynamic-update-slice_fusion), kind=kOutput, calls=%fused_computation.60 | convolution fusion | flops 283770880 | bytes 9306240 | tf_op jit(solution)/shard_map/dot_general | solution.py:21
  128.2 2.7 fusion.20
  131.0 1.6 fusion.13
  132.6 2.5 convolution_add_fusion.1
  135.3 88.9 %all-reduce.3.cloned.1.call-done = f32[32,5120]{1,0:T(8,128)} async-done(((f32[32,5120]{1,0:T(8,128)}), f32[32,5120]{1,0:T(8,128)}) %all-reduce.3.cloned.1.call-update) | async-done | bytes 655376 | tf_op jit(solution)/shard_map/psum | solution.py:63
  224.3 1.4 multiply_reduce_fusion.3
  225.6 6.5 %fusion.6 = f32[32,864]{1,0:T(8,128)S(1)} fusion(bf16[864,5120]{1,0:T(8,128)(2,1)} %param.11, bf16[32,5120]{1,0:T(8,128)(2,1)S(1)} %reshape.27, f32[5120]{0:T(1024)S(1)} %copy-done.3, f32[32,5120]{1,0:T(8,128)} %all-reduce.3.cloned.1.call-done, f32[32]{0:T(128)S(1)} %broadcast_multiply_fusion.1, f32[32]{0:T(128)S(1)} %add_sqrt_fusion, ...), kind=kOutput, calls=%fused_computation.22 | convolution fusion | flops 284753920 | bytes 10309888 | tf_op jit(solution)/shard_map/dot_general | solution.py:21
  232.2 5.3 %fusion.14 = f32[32,5120]{1,0:T(8,128)S(1)} fusion(bf16[5120,864]{0,1:T(8,128)(2,1)} %param.9, f32[32,864]{1,0:T(8,128)S(1)} %fusion.6, f32[32,864]{1,0:T(8,128)S(1)} %fusion.20, f32[32,864]{1,0:T(8,128)S(1)} %fusion.19), kind=kOutput, calls=%fused_computation.38 | convolution fusion | flops 283392000 | bytes 9834496 | tf_op jit(solution)/shard_map/dot_general | solution.py:21
  237.5 2.4 convolution_add_fusion
  240.0 91.6 %all-reduce.5.cloned.1.call-done = f32[32,5120]{1,0:T(8,128)} async-done(((f32[32,5120]{1,0:T(8,128)}), f32[32,5120]{1,0:T(8,128)}) %all-reduce.5.cloned.1.call-update) | async-done | bytes 655376 | tf_op jit(solution)/shard_map/psum | solution.py:63
  331.6 1.4 multiply_reduce_fusion.2
  333.0 2.2 multiply_reduce_fusion
  336.9 6.2 %fusion.10 = f32[32,864]{1,0:T(8,128)S(1)} fusion(bf16[864,5120]{1,0:T(8,128)(2,1)} %param.11, f32[32,5120]{1,0:T(8,128)S(1)} %fusion.4), kind=kOutput, calls=%fused_computation.25 | convolution fusion | flops 283279360 | bytes 9613312 | tf_op jit(solution)/shard_map/dot_general | solution.py:21
  343.0 6.1 %convolution_convert_fusion = bf16[864,5120]{1,0:T(8,128)(2,1)} fusion(f32[32,5120]{1,0:T(8,128)S(1)} %fusion.4, f32[32,864]{1,0:T(8,128)S(1)} %fusion.20, f32[32,864]{1,0:T(8,128)S(1)} %fusion.19), kind=kOutput, calls=%fused_computation | convolution fusion | flops 287868928 | bytes 9723904 | tf_op jit(solution)/shard_map/dot_general | solution.py:21
  349.1 6.1 %convolution_convert_fusion.2 = bf16[5120,864]{0,1:T(8,128)(2,1)} fusion(f32[32,864]{1,0:T(8,128)S(1)} %fusion.10, f32[32,864]{1,0:T(8,128)S(1)} %fusion.20, f32[32,864]{1,0:T(8,128)S(1)} %fusion.19, f32[5120]{0:T(1024)S(1)} %copy-done.2, f32[32]{0:T(128)S(1)} %add_sqrt_fusion, bf16[32,5120]{1,0:T(8,128)(2,1)S(1)} %constant_dynamic-update-slice_fusion), kind=kOutput, calls=%fused_computation.2 | convolution fusion | flops 288471040 | bytes 9527424 | tf_op jit(solution)/shard_map/dot_general | solution.py:21
  355.2 6.1 %convolution_convert_fusion.1 = bf16[5120,864]{0,1:T(8,128)(2,1)} fusion(f32[32,864]{1,0:T(8,128)S(1)} %fusion.10, f32[32,864]{1,0:T(8,128)S(1)} %fusion.19, f32[5120]{0:T(1024)S(1)} %copy-done.2, f32[32]{0:T(128)S(1)} %add_sqrt_fusion, bf16[32,5120]{1,0:T(8,128)(2,1)S(1)} %constant_dynamic-update-slice_fusion), kind=kOutput, calls=%fused_computation.1 | convolution fusion | flops 288360448 | bytes 9416832 | tf_op jit(solution)/shard_map/dot_general | solution.py:21
  (69 shorter events, 4.1 us)
Async XLA Ops:
  7.2 31.3 %copy-start.4 = (bf16[2,5120]{1,0:T(2,128)(2,1)S(1)}, bf16[2,5120]{1,0:T(2,128)(2,1)}, u32[]{:S(2)}) copy-start(bf16[2,5120]{1,0:T(2,128)(2,1)} %param.7) | copy-start | bytes 61444
  7.2 114.7 %copy-start.2 = (f32[5120]{0:T(1024)S(1)}, f32[5120]{0:T(1024)}, u32[]{:S(2)}) copy-start(f32[5120]{0:T(1024)} %param.12) | copy-start | bytes 61444
  7.2 217.1 %all-reduce.3.cloned.1.call-start = ((), (), s32[]{:S(2)}) async-start(), calls=%async_computation | async-start | bytes 1310720 | tf_op jit(solution)/shard_map/psum | solution.py:63
  7.2 31.6 %collective-permute-start = (bf16[2,5120]{1,0:T(2,128)(2,1)}, bf16[2,5120]{1,0:T(2,128)(2,1)S(1)}, u32[]{:S(2)}, u32[]{:S(2)}) collective-permute-start(bf16[2,5120]{1,0:T(2,128)(2,1)} %param.7), channel_id=1, source_target_pairs={{0,1},{1,2},{2,3},{3,4},{4,5},{5,6},{6,7},{7,8},{8,9},{9,10},{10,1... | collective-permute-start | bytes 61448 | tf_op jit(solution)/shard_map/ppermute | solution.py:16
  38.9 89.3 %copy-start = (bf16[5120,864]{0,1:T(8,128)(2,1)S(1)}, bf16[5120,864]{0,1:T(8,128)(2,1)}, u32[]{:S(2)}) copy-start(bf16[5120,864]{0,1:T(8,128)(2,1)} %param.10) | copy-start | bytes 26542084
  38.9 6.0 %collective-permute-start.1 = (bf16[2,5120]{1,0:T(2,128)(2,1)S(1)}, bf16[2,5120]{1,0:T(2,128)(2,1)S(1)}, u32[]{:S(2)}, u32[]{:S(2)}) collective-permute-start(bf16[2,5120]{1,0:T(2,128)(2,1)S(1)} %collective-permute-done), channel_id=1, source_target_pairs={{0,1},{1,2},{2,3},{3,4},{4,5},{5,6},{6,7},{7,8},{8,9},{9,10},{10,1... | collective-permute-start | bytes 61448 | tf_op jit(solution)/shard_map/ppermute | solution.py:16
  44.8 5.9 %collective-permute-start.2 = (bf16[2,5120]{1,0:T(2,128)(2,1)S(1)}, bf16[2,5120]{1,0:T(2,128)(2,1)S(1)}, u32[]{:S(2)}, u32[]{:S(2)}) collective-permute-start(bf16[2,5120]{1,0:T(2,128)(2,1)S(1)} %collective-permute-done.1), channel_id=1, source_target_pairs={{0,1},{1,2},{2,3},{3,4},{4,5},{5,6},{6,7},{7,8},{8,9},{9,10},{10,1... | collective-permute-start | bytes 61448 | tf_op jit(solution)/shard_map/ppermute | solution.py:16
  50.7 5.9 %collective-permute-start.3 = (bf16[2,5120]{1,0:T(2,128)(2,1)S(1)}, bf16[2,5120]{1,0:T(2,128)(2,1)S(1)}, u32[]{:S(2)}, u32[]{:S(2)}) collective-permute-start(bf16[2,5120]{1,0:T(2,128)(2,1)S(1)} %collective-permute-done.2), channel_id=1, source_target_pairs={{0,1},{1,2},{2,3},{3,4},{4,5},{5,6},{6,7},{7,8},{8,9},{9,10},{10,1... | collective-permute-start | bytes 61448 | tf_op jit(solution)/shard_map/ppermute | solution.py:16
  56.6 5.9 %collective-permute-start.4 = (bf16[2,5120]{1,0:T(2,128)(2,1)S(1)}, bf16[2,5120]{1,0:T(2,128)(2,1)S(1)}, u32[]{:S(2)}, u32[]{:S(2)}) collective-permute-start(bf16[2,5120]{1,0:T(2,128)(2,1)S(1)} %collective-permute-done.3), channel_id=1, source_target_pairs={{0,1},{1,2},{2,3},{3,4},{4,5},{5,6},{6,7},{7,8},{8,9},{9,10},{10,1... | collective-permute-start | bytes 61448 | tf_op jit(solution)/shard_map/ppermute | solution.py:16
  62.5 5.9 %collective-permute-start.5 = (bf16[2,5120]{1,0:T(2,128)(2,1)S(1)}, bf16[2,5120]{1,0:T(2,128)(2,1)S(1)}, u32[]{:S(2)}, u32[]{:S(2)}) collective-permute-start(bf16[2,5120]{1,0:T(2,128)(2,1)S(1)} %collective-permute-done.4), channel_id=1, source_target_pairs={{0,1},{1,2},{2,3},{3,4},{4,5},{5,6},{6,7},{7,8},{8,9},{9,10},{10,1... | collective-permute-start | bytes 61448 | tf_op jit(solution)/shard_map/ppermute | solution.py:16
  68.5 5.9 %collective-permute-start.6 = (bf16[2,5120]{1,0:T(2,128)(2,1)S(1)}, bf16[2,5120]{1,0:T(2,128)(2,1)S(1)}, u32[]{:S(2)}, u32[]{:S(2)}) collective-permute-start(bf16[2,5120]{1,0:T(2,128)(2,1)S(1)} %collective-permute-done.5), channel_id=1, source_target_pairs={{0,1},{1,2},{2,3},{3,4},{4,5},{5,6},{6,7},{7,8},{8,9},{9,10},{10,1... | collective-permute-start | bytes 61448 | tf_op jit(solution)/shard_map/ppermute | solution.py:16
  74.4 5.9 %collective-permute-start.7 = (bf16[2,5120]{1,0:T(2,128)(2,1)S(1)}, bf16[2,5120]{1,0:T(2,128)(2,1)S(1)}, u32[]{:S(2)}, u32[]{:S(2)}) collective-permute-start(bf16[2,5120]{1,0:T(2,128)(2,1)S(1)} %collective-permute-done.6), channel_id=1, source_target_pairs={{0,1},{1,2},{2,3},{3,4},{4,5},{5,6},{6,7},{7,8},{8,9},{9,10},{10,1... | collective-permute-start | bytes 61448 | tf_op jit(solution)/shard_map/ppermute | solution.py:16
  80.3 5.9 %collective-permute-start.8 = (bf16[2,5120]{1,0:T(2,128)(2,1)S(1)}, bf16[2,5120]{1,0:T(2,128)(2,1)S(1)}, u32[]{:S(2)}, u32[]{:S(2)}) collective-permute-start(bf16[2,5120]{1,0:T(2,128)(2,1)S(1)} %collective-permute-done.7), channel_id=1, source_target_pairs={{0,1},{1,2},{2,3},{3,4},{4,5},{5,6},{6,7},{7,8},{8,9},{9,10},{10,1... | collective-permute-start | bytes 61448 | tf_op jit(solution)/shard_map/ppermute | solution.py:16
  86.2 5.9 %collective-permute-start.9 = (bf16[2,5120]{1,0:T(2,128)(2,1)S(1)}, bf16[2,5120]{1,0:T(2,128)(2,1)S(1)}, u32[]{:S(2)}, u32[]{:S(2)}) collective-permute-start(bf16[2,5120]{1,0:T(2,128)(2,1)S(1)} %collective-permute-done.8), channel_id=1, source_target_pairs={{0,1},{1,2},{2,3},{3,4},{4,5},{5,6},{6,7},{7,8},{8,9},{9,10},{10,1... | collective-permute-start | bytes 61448 | tf_op jit(solution)/shard_map/ppermute | solution.py:16
  92.1 5.9 %collective-permute-start.10 = (bf16[2,5120]{1,0:T(2,128)(2,1)S(1)}, bf16[2,5120]{1,0:T(2,128)(2,1)S(1)}, u32[]{:S(2)}, u32[]{:S(2)}) collective-permute-start(bf16[2,5120]{1,0:T(2,128)(2,1)S(1)} %collective-permute-done.9), channel_id=1, source_target_pairs={{0,1},{1,2},{2,3},{3,4},{4,5},{5,6},{6,7},{7,8},{8,9},{9,10},{10,1... | collective-permute-start | bytes 61448 | tf_op jit(solution)/shard_map/ppermute | solution.py:16
  98.0 5.9 %collective-permute-start.11 = (bf16[2,5120]{1,0:T(2,128)(2,1)S(1)}, bf16[2,5120]{1,0:T(2,128)(2,1)S(1)}, u32[]{:S(2)}, u32[]{:S(2)}) collective-permute-start(bf16[2,5120]{1,0:T(2,128)(2,1)S(1)} %collective-permute-done.10), channel_id=1, source_target_pairs={{0,1},{1,2},{2,3},{3,4},{4,5},{5,6},{6,7},{7,8},{8,9},{9,10},{10,1... | collective-permute-start | bytes 61448 | tf_op jit(solution)/shard_map/ppermute | solution.py:16
  103.9 5.9 %collective-permute-start.12 = (bf16[2,5120]{1,0:T(2,128)(2,1)S(1)}, bf16[2,5120]{1,0:T(2,128)(2,1)S(1)}, u32[]{:S(2)}, u32[]{:S(2)}) collective-permute-start(bf16[2,5120]{1,0:T(2,128)(2,1)S(1)} %collective-permute-done.11), channel_id=1, source_target_pairs={{0,1},{1,2},{2,3},{3,4},{4,5},{5,6},{6,7},{7,8},{8,9},{9,10},{10,1... | collective-permute-start | bytes 61448 | tf_op jit(solution)/shard_map/ppermute | solution.py:16
  109.8 5.9 %collective-permute-start.13 = (bf16[2,5120]{1,0:T(2,128)(2,1)S(1)}, bf16[2,5120]{1,0:T(2,128)(2,1)S(1)}, u32[]{:S(2)}, u32[]{:S(2)}) collective-permute-start(bf16[2,5120]{1,0:T(2,128)(2,1)S(1)} %collective-permute-done.12), channel_id=1, source_target_pairs={{0,1},{1,2},{2,3},{3,4},{4,5},{5,6},{6,7},{7,8},{8,9},{9,10},{10,1... | collective-permute-start | bytes 61448 | tf_op jit(solution)/shard_map/ppermute | solution.py:16
  115.7 5.9 %collective-permute-start.14 = (bf16[2,5120]{1,0:T(2,128)(2,1)S(1)}, bf16[2,5120]{1,0:T(2,128)(2,1)S(1)}, u32[]{:S(2)}, u32[]{:S(2)}) collective-permute-start(bf16[2,5120]{1,0:T(2,128)(2,1)S(1)} %collective-permute-done.13), channel_id=1, source_target_pairs={{0,1},{1,2},{2,3},{3,4},{4,5},{5,6},{6,7},{7,8},{8,9},{9,10},{10,1... | collective-permute-start | bytes 61448 | tf_op jit(solution)/shard_map/ppermute | solution.py:16
  121.8 9.1 %slice-start = ((s8[8847360]{0:T(1024)(128)(4,1)}), s8[4194304]{0:T(1024)(128)(4,1)S(1)}, s32[]{:S(2)}) async-start(s8[8847360]{0:T(1024)(128)(4,1)} %bitcast.12), calls=%async_computation.2 | async-start | bytes 8388608
  121.8 9.1 %slice-start.1 = ((s8[8847360]{0:T(1024)(128)(4,1)}), s8[4194304]{0:T(1024)(128)(4,1)S(1)}, s32[]{:S(2)}) async-start(s8[8847360]{0:T(1024)(128)(4,1)} %bitcast.12), calls=%async_computation.3 | async-start | bytes 8388608
  128.2 2.7 slice-start.2
  132.6 93.0 %copy-start.3 = (f32[5120]{0:T(1024)S(1)}, f32[5120]{0:T(1024)}, u32[]{:S(2)}) copy-start(f32[5120]{0:T(1024)} %param.13) | copy-start | bytes 61444
  135.1 196.5 %all-reduce.5.cloned.1.call-start = ((), (), s32[]{:S(2)}) async-start(), calls=%async_computation.1 | async-start | bytes 1310720 | tf_op jit(solution)/shard_map/psum | solution.py:63
  225.6 11.9 %slice-start.3 = ((s8[8847360]{0:T(1024)(128)(4,1)}), s8[4194304]{0:T(1024)(128)(4,1)S(1)}, s32[]{:S(2)}) async-start(s8[8847360]{0:T(1024)(128)(4,1)} %bitcast.14), calls=%async_computation.5 | async-start | bytes 8388608
  225.6 11.9 %slice-start.4 = ((s8[8847360]{0:T(1024)(128)(4,1)}), s8[458752]{0:T(1024)(128)(4,1)S(1)}, s32[]{:S(2)}) async-start(s8[8847360]{0:T(1024)(128)(4,1)} %bitcast.14), calls=%async_computation.6 | async-start | bytes 917504
  232.2 5.3 %slice-start.5 = ((s8[8847360]{0:T(1024)(128)(4,1)}), s8[4194304]{0:T(1024)(128)(4,1)S(1)}, s32[]{:S(2)}) async-start(s8[8847360]{0:T(1024)(128)(4,1)} %bitcast.14), calls=%async_computation.7 | async-start | bytes 8388608
  237.5 95.4 %copy-start.1 = (f32[32,5120]{1,0:T(8,128)S(1)}, f32[32,5120]{1,0:T(8,128)}, u32[]{:S(2)}) copy-start(f32[32,5120]{1,0:T(8,128)} %all-reduce.3.cloned.1.call-done) | copy-start | bytes 1966084
Sparse Core Ops, SparseCore 0:
  135.2 89.0 all-reduce.2
  240.1 91.4 all-reduce.4
